TPU v7x, 128 devices: a whole 4x4x4 slice. The times are simulated.
128 devices in a mesh: field: 4 (over x_hi, core), slab: 32 (over x_lo, z, y).
Axes of the slice: x: 4 (x_hi: 2, x_lo: 2; x = x_hi * 2 + x_lo), y: 4, z: 4, core: 2. Of those that a mesh axis runs over, the one named last changes fastest.
Arguments:
- velocity_u: float32 [512, 512, 512], P('field', 'slab'), may hold values from -6 to 6
- velocity_v: float32 [512, 512, 512], P('field', 'slab'), may hold values from -6 to 6
- scalar_theta: float32 [512, 512, 512], P('field', 'slab'), may hold values from -6 to 6
Outputs:
- spectrum: float32 [4, 320, 320, 320], P('field', 'slab')
All inputs are finite; a program needn't handle non-finite values.
Results may differ from a plain program's by a relative error of at most 0.00029.
Values sent between devices are 32-bit elements; how exact they have to be, the bound alone decides.
A program may use at most 128 MiB of HBM per device.

v0:
```python
import jax
import jax.numpy as jnp
from jax import lax
from jax.sharding import PartitionSpec as P

N = 512
KEEP = 160


HIGH = lax.Precision.HIGHEST


def grouped_exchange(value, axis, split_dim, concat_dim, work, item_dim, out_dim):
    items = jax.tree.leaves(value)[0].shape[item_dim]
    count = 2 if items % 2 == 0 else 1
    finished = []
    for k in range(count):
        group = jax.tree.map(
            lambda a: lax.slice_in_dim(
                a, k * (items // count), (k + 1) * (items // count), axis=item_dim
            ),
            value,
        )
        finished.append(
            work(
                lax.all_to_all(
                    group, axis, split_axis=split_dim, concat_axis=concat_dim, tiled=True
                )
            )
        )
    return jax.tree.map(lambda *parts: jnp.concatenate(parts, axis=out_dim), *finished)


def depth_table():
    places = jnp.arange(N, dtype=jnp.int32)
    waves = jnp.arange(KEEP, dtype=jnp.int32)
    phase = places[:, None] * waves[None, :] % N
    angle = phase.astype(jnp.float32) * (2.0 * jnp.pi / N)
    norm = 1.0 / jnp.sqrt(jnp.float32(N))
    return jnp.concatenate([jnp.cos(angle), -jnp.sin(angle)], axis=1) * norm


def plane_table():
    places = jnp.arange(N, dtype=jnp.int32)
    waves = jnp.arange(2 * KEEP, dtype=jnp.int32) - KEEP
    phase = waves[:, None] * places[None, :] % N
    angle = phase.astype(jnp.float32) * (2.0 * jnp.pi / N)
    norm = 1.0 / jnp.sqrt(jnp.float32(N))
    return jnp.concatenate([jnp.cos(angle), jnp.sin(angle)], axis=0) * norm


def combine(cos_part, sin_part):
    real_part = cos_part[..., :KEEP] + sin_part[..., KEEP:]
    imag_part = cos_part[..., KEEP:] - sin_part[..., :KEEP]
    return jnp.concatenate([real_part, imag_part], axis=-1)


def depth_form(values):
    return jnp.einsum("axyz,zc->axyc", values, depth_table(), precision=HIGH)


def first_form(piece):
    mixed = jnp.einsum("jx,axyc->ajyc", plane_table(), piece, precision=HIGH)
    return combine(mixed[:, : 2 * KEEP], mixed[:, 2 * KEEP :])


def second_form(piece):
    mixed = jnp.einsum("jy,akyc->akjc", plane_table(), piece, precision=HIGH)
    return combine(mixed[:, :, : 2 * KEEP], mixed[:, :, 2 * KEEP :])


def shards(velocity_u, velocity_v, scalar_theta):
    products = jnp.stack(
        [
            velocity_u * velocity_u,
            velocity_v * velocity_v,
            velocity_u * velocity_v,
            velocity_u * scalar_theta,
        ],
        axis=0,
    )
    partial_spec = depth_form(products)
    planes = grouped_exchange(partial_spec, "field", 0, 1, first_form, 2, 2)
    result = second_form(lax.all_to_all(planes, "slab", split_axis=1, concat_axis=2, tiled=True))
    local_rows = result.shape[1]
    first_index = lax.axis_index("slab") * local_rows + jnp.arange(local_rows, dtype=jnp.int32)
    second_index = jnp.arange(2 * KEEP, dtype=jnp.int32)
    column_index = jnp.arange(2 * KEEP, dtype=jnp.int32)
    zero_mode = (
        (first_index[:, None, None] == KEEP)
        & (second_index[None, :, None] == KEEP)
        & (column_index[None, None, :] == 0)
    )
    return jnp.where(zero_mode[None], jnp.float32(0.0), result)


def solution(mesh):
    in_specs = (P("field", "slab", None), P("field", "slab", None), P("field", "slab", None))
    out_specs = P("field", "slab", None, None)
    return jax.shard_map(shards, mesh=mesh, in_specs=in_specs, out_specs=out_specs, check_vma=False)
```

profile of v0, /device:TPU:22, one launch (start us, length us, event | category | flops | bytes accessed | tf_op | source)
XLA Modules:
  0.0 392.9 jit_solution(5173919117945034792)
XLA Ops:
  0.0 1.3 sine_negate_fusion
  1.3 17.5 %multiply_bitcast_fusion.2 = (f32[1,128,16,512]{3,1,2,0:T(8,128)}, f32[1,128,16,512]{3,1,2,0:T(8,128)}, f32[1,128,16,512]{3,1,2,0:T(8,128)}, f32[1,128,16,512]{3,1,2,0:T(8,128)}) fusion(f32[128,16,512]{2,1,0:T(8,128)} %param.3, f32[128,16,512]{2,1,0:T(8,128)} %param.4, f32[128,16,512]{2,1,0:T(8,128)} %param.5), kind=kLoop, calls=%fused_computation.20 | loop fusion | flops 4194304 | bytes 29360128 | tf_op jit(solution)/shard_map/stack | solution.py:73
  18.8 22.2 %fusion = f32[4,128,16,320]{1,3,2,0:T(8,128)} fusion(f32[1,128,16,512]{3,1,2,0:T(8,128)} %get-tuple-element.16, f32[1,128,16,512]{3,1,2,0:T(8,128)} %get-tuple-element.14, f32[1,128,16,512]{3,1,2,0:T(8,128)} %get-tuple-element.15, f32[1,128,16,512]{3,1,2,0:T(8,128)} %get-tuple-element.13, f32[512,160]{0,1:T(8,128)S(1)} %get-tuple-element.19, ...), kind=kOutput, calls=%fused_computation | convolution fusion | flops 16119037952 | bytes 27918336 | tf_op jit(solution)/shard_map/axyz,zc->axyc/dot_general | solution.py:59
  41.0 7.4 %fusion.56 = (f32[4,128,8,320]{1,3,2,0:T(8,128)S(1)}, f32[4,128,8,320]{1,3,2,0:T(8,128)}) fusion(f32[4,128,16,320]{1,3,2,0:T(8,128)} %fusion), kind=kLoop, calls=%fused_computation.75 | loop fusion | bytes 20971520 | tf_op jit(solution)/shard_map/slice | solution.py:19
  48.4 62.7 %all_to_all.33 = f32[4,128,8,320]{1,3,2,0:T(8,128)} all-to-all(f32[4,128,8,320]{1,3,2,0:T(8,128)S(1)} %get-tuple-element.5), channel_id=1, replica_groups=mesh['field'=4,'slab'=32] {'field'}, dimensions={0} | all-to-all | bytes 10485760 | tf_op jit(solution)/shard_map/all_to_all | solution.py:26
  111.1 8.2 %all-to-all-start.1 = ((f32[4,128,8,320]{1,3,2,0:T(8,128)}), f32[4,128,8,320]{1,3,2,0:T(8,128)}, u32[]{:S(2)}, u32[]{:S(2)}) async-start(f32[4,128,8,320]{1,3,2,0:T(8,128)} %get-tuple-element.6), calls=%async_computation.1 | async-start | bytes 10485760 | tf_op jit(solution)/shard_map/all_to_all | solution.py:26
  119.3 2.6 fusion.42
  121.9 15.5 %fusion.15 = f32[1,640,8,320]{1,3,2,0:T(8,128)S(1)} fusion(f32[320,512]{1,0:T(8,128)S(1)} %get-tuple-element.18, f32[320,512]{1,0:T(8,128)S(1)} %get-tuple-element.17, f32[4,128,8,320]{1,3,2,0:T(8,128)} %all_to_all.33), kind=kOutput, calls=%fused_computation.22 | convolution fusion | flops 10066984960 | bytes 13107200 | tf_op jit(solution)/shard_map/jx,axyc->ajyc/dot_general | solution.py:63
  137.4 2.4 slice_add_fusion.2
  139.8 37.3 %all-to-all-done.1 = f32[4,128,8,320]{1,3,2,0:T(8,128)} async-done(((f32[4,128,8,320]{1,3,2,0:T(8,128)}), f32[4,128,8,320]{1,3,2,0:T(8,128)}, u32[]{:S(2)}, u32[]{:S(2)}) %all-to-all-start.1) | async-done | bytes 5242912 | tf_op jit(solution)/shard_map/all_to_all | solution.py:26
  177.1 15.6 %fusion.18 = f32[1,640,8,320]{1,3,2,0:T(8,128)S(1)} fusion(f32[320,512]{1,0:T(8,128)S(1)} %get-tuple-element.18, f32[320,512]{1,0:T(8,128)S(1)} %get-tuple-element.17, f32[4,128,8,320]{1,3,2,0:T(8,128)} %all-to-all-done.1), kind=kOutput, calls=%fused_computation.23 | convolution fusion | flops 10066984960 | bytes 13107200 | tf_op jit(solution)/shard_map/jx,axyc->ajyc/dot_general | solution.py:63
  192.8 3.0 slice_add_fusion.1
  195.8 6.5 %maximum_maximum_fusion = f32[1,320,16,320]{1,3,2,0:T(8,128)} fusion(f32[1,320,8,160]{1,3,2,0:T(8,128)} %get-tuple-element.12, f32[1,320,8,160]{1,3,2,0:T(8,128)} %get-tuple-element.11, f32[1,320,8,160]{1,3,2,0:T(8,128)} %get-tuple-element.10, f32[1,320,8,160]{1,3,2,0:T(8,128)S(1)} %get-tuple-element.9), kind=kLoop, calls=%fused_computation.8 | loop fusion | flops 4915200 | bytes 13107200 | tf_op jit(solution)/shard_map/concatenate | solution.py:31
  202.2 9.0 %copy.38 = f32[1,320,16,320]{3,2,0,1:T(8,128)} copy(f32[1,320,16,320]{1,3,2,0:T(8,128)} %maximum_maximum_fusion) | data formatting | bytes 13107200 | tf_op jit(solution)/shard_map/concatenate | solution.py:31
  211.2 9.4 %all-to-all-start.2 = ((f32[1,320,16,320]{3,2,0,1:T(8,128)}), f32[1,320,16,320]{3,2,0,1:T(8,128)}, u32[]{:S(2)}, u32[]{:S(2)}) async-start(f32[1,320,16,320]{3,2,0,1:T(8,128)} %copy.38), calls=%async_computation.2 | async-start | bytes 15728640 | tf_op jit(solution)/shard_map/all_to_all | solution.py:84
  220.7 0.1 broadcast_and_fusion
  220.7 120.1 %all-to-all-done.2 = f32[1,320,16,320]{3,2,0,1:T(8,128)} async-done(((f32[1,320,16,320]{3,2,0,1:T(8,128)}), f32[1,320,16,320]{3,2,0,1:T(8,128)}, u32[]{:S(2)}, u32[]{:S(2)}) %all-to-all-start.2) | async-done | bytes 6553632 | tf_op jit(solution)/shard_map/all_to_all | solution.py:84
  340.8 4.0 %copy.39 = f32[1,10,32,16,320]{4,3,2,1,0:T(8,128)S(1)} copy(f32[1,10,32,16,320]{4,3,1,2,0:T(8,128)} %bitcast.14) | data formatting | bytes 13107200 | tf_op jit(solution)/shard_map/all_to_all | solution.py:84
  344.8 37.3 %convolution_bitcast_fusion = f32[1,10,640,320]{2,3,1,0:T(8,128)S(1)} fusion(f32[10,512,320]{2,1,0:T(8,128)S(1)} %bitcast.53, f32[320,512]{1,0:T(8,128)S(1)} %get-tuple-element.18, f32[320,512]{1,0:T(8,128)S(1)} %get-tuple-element.17), kind=kOutput, calls=%fused_computation.21 | convolution fusion | flops 12583567360 | bytes 16056320 | tf_op jit(solution)/shard_map/jy,akyc->akjc/dot_general | solution.py:68
  382.1 1.3 slice_add_fusion
  383.4 2.9 maximum_select_fusion
  386.3 6.2 %copy.41 = f32[1,10,320,320]{3,2,1,0:T(8,128)} copy(f32[1,10,320,320]{2,3,1,0:T(8,128)} %maximum_select_fusion) | data formatting | bytes 8192000 | tf_op jit(solution)/shard_map/jit(_where)/select_n | solution.py:94
  (4 shorter events, 0.0 us)
Async XLA Ops:
  111.1 66.0 %all-to-all-start.1 = ((f32[4,128,8,320]{1,3,2,0:T(8,128)}), f32[4,128,8,320]{1,3,2,0:T(8,128)}, u32[]{:S(2)}, u32[]{:S(2)}) async-start(f32[4,128,8,320]{1,3,2,0:T(8,128)} %get-tuple-element.6), calls=%async_computation.1 | async-start | bytes 10485760 | tf_op jit(solution)/shard_map/all_to_all | solution.py:26
  211.2 129.6 %all-to-all-start.2 = ((f32[1,320,16,320]{3,2,0,1:T(8,128)}), f32[1,320,16,320]{3,2,0,1:T(8,128)}, u32[]{:S(2)}, u32[]{:S(2)}) async-start(f32[1,320,16,320]{3,2,0,1:T(8,128)} %copy.38), calls=%async_computation.2 | async-start | bytes 15728640 | tf_op jit(solution)/shard_map/all_to_all | solution.py:84
where the time goes:
time: 401 us; the launch traced here: 393 us
  waiting for transfers between devices  157 us (39%)
  matrix products  90.5 us (23%)
  blocking collectives  62.7 us (16%)
  other arithmetic  37.7 us (9%)
  local copies, waits for them, and re-layouts  26.6 us (7%)
  starting transfers between devices  17.6 us (4%)
    all_to_all x1, waiting for transfers between devices, shards(): lax.all_to_all(planes, 'slab', split_axis=1, concat_axis=2, tiled=True)  120 us
    all_to_all x1, blocking collectives, grouped_exchange(): lax.all_to_all(group, axis, split_axis=split_dim, concat_axis=concat_dim,...  62.7 us
    all_to_all x1, waiting for transfers between devices, grouped_exchange(): lax.all_to_all(group, axis, split_axis=split_dim, concat_axis=concat_dim,...  37.3 us
    dot_general x1, matrix products, second_form(): mixed = jnp.einsum('jy,akyc->akjc', plane_table(), piece, precision=HIGH)  37.3 us
    dot_general x2, matrix products, first_form(): mixed = jnp.einsum('jx,axyc->ajyc', plane_table(), piece, precision=HIGH)  31.1 us
    dot_general x1, matrix products, depth_form(): return jnp.einsum('axyz,zc->axyc', values, depth_table(), precision=HIGH)  22.2 us
    another operation x1, other arithmetic, shards(): jnp.stack([velocity_u * velocity_u, velocity_v * velocity_v, velocity_u *...  17.5 us
    all_to_all x1, starting transfers between devices, shards(): lax.all_to_all(planes, 'slab', split_axis=1, concat_axis=2, tiled=True)  9.39 us
  transfers between devices with their start and end apart: 2, of which 2 were waited for; matrix products, arithmetic and copies ran while one was open for 5% of the time, Pallas kernels for 0%

commit v1 on v0

v1 whole, which is shorter than its diff:
```python
import functools

import jax
import jax.numpy as jnp
import numpy as np
from jax import lax
from jax.experimental import pallas as pl
from jax.experimental.pallas import tpu as pltpu
from jax.sharding import PartitionSpec as P

N = 512
KEEP = 160
MESH = pl.DeviceIdType.MESH
F32 = jnp.float32
BF16 = jnp.bfloat16
PITCH = 328
MIX_PITCH = 168
FACTORS = ((0, 0), (1, 1), (0, 1), (0, 2))


def split_table(table):
    high = table.astype(BF16)
    low = (table - high.astype(np.float64)).astype(BF16)
    return high, low


def waves(k, x):
    angle = (np.outer(k, x) % N) * (2.0 * np.pi / N)
    return np.cos(angle) / np.sqrt(N), np.sin(angle) / np.sqrt(N)


def depth_tables():
    cos, sin = waves(np.arange(KEEP), np.arange(N))
    real, imag = cos.T, -sin.T
    tables = np.zeros((2, N, 512))
    for parity in range(2):
        tables[parity, :, 0:128] = real[:, :128]
        tables[parity, :, 128:256] = imag[:, :128]
        at = 256 + 64 * parity
        tables[parity, :, at : at + 32] = real[:, 128:]
        tables[parity, :, at + 32 : at + 64] = imag[:, 128:]
        tables[parity, :, at + 128 : at + 160] = imag[:, 128:]
        tables[parity, :, at + 160 : at + 192] = -real[:, 128:]
    return split_table(tables)


def first_tables():
    tables = np.zeros((2, 640, 256))
    for half in range(2):
        x = np.arange(256) + 256 * half
        for side in range(2):
            cos, sin = waves(np.arange(KEEP) - KEEP * (1 - side), x)
            tables[half, side * 320 : side * 320 + 160] = cos
            tables[half, side * 320 + 160 : side * 320 + 320] = sin
    return split_table(tables)


def second_tables():
    tables = np.zeros((2, 2, 320, 256))
    y = np.arange(256)
    mixed = np.concatenate([2 * np.arange(128), 2 * np.arange(128) + 1])
    for parity in range(2):
        k = 2 * np.arange(KEEP) + parity - KEEP
        for order, places in enumerate((y, mixed)):
            cos, sin = waves(k, places)
            tables[parity, order] = np.concatenate([cos, sin], axis=0)
    return split_table(tables)


def halves(value):
    high = value.astype(BF16)
    return high, (value - high.astype(F32)).astype(BF16)


def dot(a, b):
    return jnp.dot(a, b, preferred_element_type=F32)


def exchange_kernel(
    u, v, t, zh, zl, xh, xl, ymain, ymix,
    fields, stack, zbuf, zout, xs, xr, xsm, xrm, dmain, dmix,
    in_sem, zs_sem, zr_sem, xs_sem, xr_sem, ds_sem, dr_sem, dl_sem,
):
    field, slab = lax.axis_index("field"), lax.axis_index("slab")
    hi, core = field // 2, field % 2
    lo, plane = slab // 16, slab % 16

    def peer_x(rel):
        half, side = (hi + rel // 2) % 2, (lo + rel % 2) % 2
        return half, side, {"field": half * 2 + core, "slab": side * 16 + plane}

    def peer_plane(step):
        other = (plane + step) % 16
        return other, {"field": field, "slab": lo * 16 + other}

    partner = {"field": hi * 2 + (1 - core), "slab": slab}
    loads = [
        pltpu.make_async_copy(ref.at[:, pl.ds(128 * part, 128)], fields.at[i, part], in_sem.at[i, part])
        for i, ref in enumerate((u, v, t))
        for part in range(4)
    ]
    for load in loads:
        load.start()

    barrier = pltpu.get_barrier_semaphore()
    pl.semaphore_signal(barrier, 1, device_id=partner, device_id_type=MESH)
    for rel in range(1, 4):
        pl.semaphore_signal(barrier, 1, device_id=peer_x(rel)[2], device_id_type=MESH)

    def greet(step, carry):
        pl.semaphore_signal(barrier, 1, device_id=peer_plane(step)[1], device_id_type=MESH)
        return carry

    lax.fori_loop(1, 16, greet, 0)
    pl.semaphore_wait(barrier, 19)
    for load in loads:
        load.wait()

    def z_copy(chunk):
        return pltpu.make_async_remote_copy(
            src_ref=zout.at[chunk % 6],
            dst_ref=zbuf.at[chunk, :, pl.ds(pl.multiple_of(core * 128, 128), 128), :],
            send_sem=zs_sem.at[chunk],
            recv_sem=zr_sem.at[chunk],
            device_id=partner,
            device_id_type=MESH,
        )

    def put_z(chunk, value):
        rows = pl.ds(pl.multiple_of(core * 128, 128), 128)
        for half in range(2):
            zbuf[chunk, half, rows, :] = value[half * 128 : half * 128 + 128]
            zout[chunk % 6, half] = value[256 + half * 128 : 384 + half * 128]
        z_copy(chunk).start()

    def depth_pair(pair):
        tail = None
        for parity in range(2):
            y = 2 * pair + parity
            for part in range(4):
                values = [fields[i, part, pl.ds(y, 128, stride=16), :] for i in range(3)]
                columns = slice(part * 128, part * 128 + 128)
                for product, (a, b) in enumerate(FACTORS):
                    high, low = halves(values[a] * values[b])
                    row = (product + core) % 2 * 256 + product // 2 * 128
                    stack[pl.ds(pl.multiple_of(row, 128), 128), columns] = high
                    stack[pl.ds(pl.multiple_of(row + 512, 128), 128), columns] = low
            both = dot(stack[...], zh[parity])
            value = both[:512] + both[512:] + dot(stack[:512], zl[parity])

            @pl.when(pair >= 2)
            def _():
                z_copy(3 * (pair - 2) + parity).wait_send()

            put_z(3 * pair + parity, value[:, :256])
            tail = value[:, 256:] if tail is None else tail + value[:, 256:]

        @pl.when(pair >= 2)
        def _():
            z_copy(3 * (pair - 2) + 2).wait_send()

        put_z(3 * pair + 2, tail)

    def first(chunk):
        z_copy(chunk).wait_recv()
        sides = []
        for half in range(2):
            high, low = halves(zbuf[chunk, half])
            mixed = dot(xh[hi], high) + dot(xh[hi], low) + dot(xl[hi], high)
            for side in range(2):
                sides.append((half, side, mixed[side * 320 : side * 320 + 160], mixed[side * 320 + 160 : side * 320 + 320]))
        return sides

    def main_rows(item):
        return pl.ds(pl.multiple_of(item * PITCH, 8), 320)

    def mix_rows(item):
        return pl.ds(pl.multiple_of(item * MIX_PITCH, 8), 160)

    def x_copy(rel, y):
        half, side, device = peer_x(rel)
        return pltpu.make_async_remote_copy(
            src_ref=xs.at[main_rows((half * 2 + side) * 16 + y), :],
            dst_ref=xr.at[main_rows((rel - 1) * 16 + y), :],
            send_sem=xs_sem.at[rel - 1, y],
            recv_sem=xr_sem.at[rel - 1, y],
            device_id=device,
            device_id_type=MESH,
        )

    def xm_copy(rel, pair):
        half, side, device = peer_x(rel)
        return pltpu.make_async_remote_copy(
            src_ref=xsm.at[mix_rows((half * 2 + side) * 8 + pair), :],
            dst_ref=xrm.at[mix_rows((rel - 1) * 8 + pair), :],
            send_sem=xs_sem.at[rel - 1, 16 + pair],
            recv_sem=xr_sem.at[rel - 1, 16 + pair],
            device_id=device,
            device_id_type=MESH,
        )

    def first_main(pair, parity):
        y = 2 * pair + parity
        for half, side, cos, sin in first(3 * pair + parity):
            rows = main_rows((half * 2 + side) * 16 + y)
            real = cos[:, :128] + sin[:, 128:]
            imag = cos[:, 128:] - sin[:, :128]
            xs[rows, :] = jnp.concatenate([real, imag], axis=0)
        for rel in (2, 1, 3):
            x_copy(rel, y).start()

    def first_mix(pair):
        for half, side, cos, sin in first(3 * pair + 2):
            xsm[mix_rows((half * 2 + side) * 8 + pair), :] = cos[:, :128] + sin[:, 128:]
        for rel in (2, 1, 3):
            xm_copy(rel, pair).start()

    def produce(pair, carry):
        depth_pair(pair)
        first_main(pair, 0)
        first_main(pair, 1)
        return carry

    lax.fori_loop(0, 8, produce, 0)

    def produce_mix(pair, carry):
        first_mix(pair)
        return carry

    lax.fori_loop(0, 8, produce_mix, 0)

    own = hi * 2 + lo

    def d_copy(group, block, step, device, other):
        near = (lo + block) % 2
        if group < 2:
            row = near * 256 + plane * 16 + group * 8
            src = dmain.at[block * 2 + group, pl.ds(other * 10, 10)]
            dst = ymain.at[:, pl.ds(pl.multiple_of(row, 8), 8), :]
        else:
            row = near * 128 + plane * 8
            src = dmix.at[block, pl.ds(other * 10, 10)]
            dst = ymix.at[:, pl.ds(pl.multiple_of(row, 8), 8), :]
        item = group * 2 + block
        if device is None:
            return pltpu.make_async_copy(src, dst, dl_sem.at[item])
        return pltpu.make_async_remote_copy(
            src_ref=src, dst_ref=dst, send_sem=ds_sem.at[item], recv_sem=dr_sem.at[item],
            device_id=device, device_id_type=MESH,
        )

    def send_group(group):
        for block in range(2):
            def go(step, carry):
                other, device = peer_plane(step)
                d_copy(group, block, step, device, other).start()
                return carry

            lax.fori_loop(1, 16, go, 0)
            d_copy(group, block, 0, None, plane).start()

    for group in range(2):
        for rel in range(1, 4):
            def arrive(y, carry):
                x_copy(rel, y).wait_recv()
                return carry

            lax.fori_loop(group * 8, group * 8 + 8, arrive, 0)

        def turn(k, carry):
            for part in range(2):
                base = group * 8 * PITCH + part * 160 + k
                columns = slice(part * 128, part * 128 + 128)

                def take(ref, item):
                    return ref[pl.ds(item * 16 * PITCH + base, 8, stride=PITCH), :]

                dmain[group, k, :, columns] = take(xs, own) + take(xr, 1)
                dmain[2 + group, k, :, columns] = take(xr, 0) + take(xr, 2)
            return carry

        lax.fori_loop(0, 160, turn, 0)
        send_group(group)

    for rel in range(1, 4):
        def arrive_mix(pair, carry):
            xm_copy(rel, pair).wait_recv()
            return carry

        lax.fori_loop(0, 8, arrive_mix, 0)

    def turn_mix(k, carry):
        def take(ref, item):
            return ref[pl.ds(item * 8 * MIX_PITCH + k, 8, stride=MIX_PITCH), :]

        dmix[0, k] = take(xsm, own) + take(xrm, 1)
        dmix[1, k] = take(xrm, 0) + take(xrm, 2)
        return carry

    lax.fori_loop(0, 160, turn_mix, 0)
    send_group(2)

    for chunk in range(18, 24):
        z_copy(chunk).wait_send()
    for rel in range(1, 4):
        def left(y, carry):
            x_copy(rel, y).wait_send()
            return carry

        lax.fori_loop(0, 16, left, 0)

        def left_mix(pair, carry):
            xm_copy(rel, pair).wait_send()
            return carry

        lax.fori_loop(0, 8, left_mix, 0)
    for group in range(3):
        for block in range(2):
            item = group * 2 + block
            whole = (dmain.at[block * 2 + group] if group < 2 else dmix.at[block]).at[pl.ds(0, 150)]
            pltpu.make_async_copy(whole, whole, ds_sem.at[item]).wait()
            pltpu.make_async_copy(whole, whole, dr_sem.at[item]).wait()
            d_copy(group, block, 0, None, plane).wait()


def exchange(u, v, t):
    zh, zl = depth_tables()
    xh, xl = first_tables()
    any_space = pl.BlockSpec(memory_space=pl.ANY)
    vmem = pl.BlockSpec(memory_space=pltpu.VMEM)
    return pl.pallas_call(
        exchange_kernel,
        out_shape=(
            jax.ShapeDtypeStruct((10, 512, 256), F32),
            jax.ShapeDtypeStruct((10, 256, 128), F32),
        ),
        in_specs=[any_space] * 3 + [vmem] * 4,
        out_specs=(any_space, any_space),
        scratch_shapes=[
            pltpu.VMEM((3, 4, 2048, 128), F32),
            pltpu.VMEM((1024, 512), BF16),
            pltpu.VMEM((24, 2, 256, 256), F32),
            pltpu.VMEM((6, 2, 128, 256), F32),
            pltpu.VMEM((4 * 16 * PITCH, 128), F32),
            pltpu.VMEM((3 * 16 * PITCH, 128), F32),
            pltpu.VMEM((4 * 8 * MIX_PITCH, 128), F32),
            pltpu.VMEM((3 * 8 * MIX_PITCH, 128), F32),
            pltpu.VMEM((4, 160, 8, 256), F32),
            pltpu.VMEM((2, 160, 8, 128), F32),
            pltpu.SemaphoreType.DMA((3, 4)),
            pltpu.SemaphoreType.DMA((24,)),
            pltpu.SemaphoreType.DMA((24,)),
            pltpu.SemaphoreType.DMA((3, 24)),
            pltpu.SemaphoreType.DMA((3, 24)),
            pltpu.SemaphoreType.DMA((6,)),
            pltpu.SemaphoreType.DMA((6,)),
            pltpu.SemaphoreType.DMA((6,)),
        ],
        compiler_params=pltpu.CompilerParams(
            collective_id=0, has_side_effects=True, vmem_limit_bytes=67043328
        ),
        name="exchange",
    )(u.reshape(2048, 512), v.reshape(2048, 512), t.reshape(2048, 512), zh, zl, xh, xl)


def second_kernel(main, mix, fh, fl, out, rows):
    slab = lax.axis_index("slab")
    row = slab * 10 + pl.program_id(0)
    low_y, high_y = main[0, :256, :], main[0, 256:, :]
    low_m, high_m = mix[0, :128, :], mix[0, 128:, :]
    for parity in range(2):
        if parity == 0:
            part, tail = low_y + high_y, low_m + high_m
        else:
            part, tail = low_y - high_y, low_m - high_m
        tail = jnp.concatenate([tail, pltpu.roll(tail, 64, 1)], axis=0)
        outs = []
        for order, value in ((0, part), (1, tail)):
            high, low = halves(value)
            a, b = fh[parity, order], fl[parity, order]
            outs.append(dot(a, high) + dot(a, low) + dot(b, high))
        wide, slim = outs
        cos, sin = wide[:160], wide[160:]
        real = cos[:, :128] + sin[:, 128:]
        imag = cos[:, 128:] - sin[:, :128]
        cos, sin = slim[:160], slim[160:]
        tail_real = cos + pltpu.roll(sin, 96, 1)
        tail_imag = cos - pltpu.roll(sin, 32, 1)
        result = jnp.concatenate(
            [real, tail_real[:, :32], imag, tail_imag[:, 32:64], jnp.zeros((160, 64), F32)], axis=1
        )
        if parity == 0:
            at_row = lax.broadcasted_iota(jnp.int32, (160, 384), 0)
            at_col = lax.broadcasted_iota(jnp.int32, (160, 384), 1)
            zero = (at_row == 80) & (at_col == 0) & (row == KEEP)
            result = jnp.where(zero, 0.0, result)
        for part in range(3):
            rows[part, pl.ds(parity, 160, stride=2), :] = result[:, part * 128 : part * 128 + 128]
    out[0, 0, :, :128] = rows[0]
    out[0, 0, :, 128:256] = rows[1]
    out[0, 0, :, 256:] = rows[2, :, :64]


def second(main, mix):
    fh, fl = second_tables()
    whole = pl.BlockSpec((2, 2, 320, 256), lambda i: (0, 0, 0, 0))
    return pl.pallas_call(
        second_kernel,
        grid=(10,),
        out_shape=jax.ShapeDtypeStruct((1, 10, 320, 320), F32),
        in_specs=[
            pl.BlockSpec((1, 512, 256), lambda i: (i, 0, 0)),
            pl.BlockSpec((1, 256, 128), lambda i: (i, 0, 0)),
            whole,
            whole,
        ],
        out_specs=pl.BlockSpec((1, 1, 320, 320), lambda i: (0, i, 0, 0)),
        scratch_shapes=[pltpu.VMEM((3, 320, 128), F32)],
        compiler_params=pltpu.CompilerParams(dimension_semantics=("arbitrary",)),
        name="second",
    )(main, mix, fh, fl)


def shards(velocity_u, velocity_v, scalar_theta):
    main, mix = exchange(velocity_u, velocity_v, scalar_theta)
    return second(main, mix)


def solution(mesh):
    spec = P("field", "slab", None)
    return jax.shard_map(
        shards,
        mesh=mesh,
        in_specs=(spec, spec, spec),
        out_specs=P("field", "slab", None, None),
        check_vma=False,
    )
```

time: 401 us -> 194 us (0.48)
  the two profiles are of different devices: /device:TPU:22 before, /device:TPU:0 now
where the time goes in v1:
time: 194 us
  Pallas kernels  194 us (100%)
    pallas_call x1, Pallas kernels, exchange(): pl.pallas_call(exchange_kernel, out_shape=(jax.ShapeDtypeStruct((10, 512,...  181 us
    pallas_call x1, Pallas kernels, second(): pl.pallas_call(second_kernel, grid=(10,), out_shape=jax.ShapeDtypeStruct(...  12.5 us

profile of v1, /device:TPU:0, one launch (start us, length us, event | category | flops | bytes accessed | tf_op | source)
XLA Modules:
  0.0 193.5 jit_solution(16622696128959389372)
XLA Ops:
  0.0 181.0 %exchange.1 = (f32[10,512,256]{2,1,0:T(8,128)}, f32[10,256,128]{2,1,0:T(8,128)}) custom-call(f32[2048,512]{1,0:T(8,128)} %bitcast.3, f32[2048,512]{1,0:T(8,128)} %bitcast.4, f32[2048,512]{1,0:T(8,128)} %bitcast.5, bf16[2,512,512]{2,1,0:T(8,128)(2,1)} %constant.12.clone.zh, bf16[2,512,512]{2,1,0:T(8,128)(2,1)} %constant.13.clone.zl, ...), custom_call_target="tpu_custom_call" | custom-call | tf_op jit(solution)/shard_map/exchange/pallas_call | solution.py:331
  181.0 12.5 %second.1 = f32[1,10,320,320]{3,2,1,0:T(8,128)} custom-call(f32[10,512,256]{2,1,0:T(8,128)} %get-tuple-element.7.main, f32[10,256,128]{2,1,0:T(8,128)} %get-tuple-element.8.mix, bf16[2,2,320,256]{3,2,1,0:T(8,128)(2,1)} %constant.16.clone.fh, bf16[2,2,320,256]{3,2,1,0:T(8,128)(2,1)} %constant.17.clone.fl), custom_call_target="tpu_custom_call" | custom-call | tf_op jit(solution)/shard_map/second/pallas_call | solution.py:407

commit v2 on v0

v2 whole, which is shorter than its diff:
```python
import functools

import jax
import jax.numpy as jnp
import numpy as np
from jax import lax
from jax.experimental import pallas as pl
from jax.experimental.pallas import tpu as pltpu
from jax.sharding import PartitionSpec as P

N = 512
KEEP = 160
MESH = pl.DeviceIdType.MESH
F32 = jnp.float32
BF16 = jnp.bfloat16
GROUPS = (4, 3, 1, 1, 1)
STARTS = (0, 4, 7, 8, 9)
STEPS = (
    ((0, 1), (1, 0), (0, 3), (3, 0), (1, 1), (3, 3), (1, 3), (3, 1))
    + ((2, 1), (2, 3), (0, 2), (2, 0), (2, 2))
    + ((1, 2), (3, 2))
)
PITCH = 328
MIX_PITCH = 168
FACTORS = ((0, 0), (1, 1), (0, 1), (0, 2))


def split_table(table):
    high = table.astype(BF16)
    low = (table - high.astype(np.float64)).astype(BF16)
    return high, low


def waves(k, x):
    angle = (np.outer(k, x) % N) * (2.0 * np.pi / N)
    return np.cos(angle) / np.sqrt(N), np.sin(angle) / np.sqrt(N)


def depth_tables():
    cos, sin = waves(np.arange(KEEP), np.arange(N))
    real, imag = cos.T, -sin.T
    tables = np.zeros((3, N, 256))
    tables[0, :, :128] = real[:, :128]
    tables[0, :, 128:] = imag[:, :128]
    for parity in range(2):
        at = 64 * parity
        tables[1 + parity, :, at : at + 32] = real[:, 128:]
        tables[1 + parity, :, at + 32 : at + 64] = imag[:, 128:]
        tables[1 + parity, :, at + 128 : at + 160] = imag[:, 128:]
        tables[1 + parity, :, at + 160 : at + 192] = -real[:, 128:]
    return split_table(tables)


def first_tables():
    order = (10 * np.arange(16)[None, :] + np.arange(11)[:, None]).reshape(-1)
    tables = np.zeros((2, 352, 256))
    for half in range(2):
        tables[half] = np.concatenate(waves(order, np.arange(256) + 256 * half), axis=0)
    return split_table(tables)


def second_tables():
    tables = np.zeros((2, 2, 320, 256))
    y = np.arange(256)
    mixed = np.concatenate([2 * np.arange(128), 2 * np.arange(128) + 1])
    for parity in range(2):
        k = 2 * np.arange(KEEP) + parity - KEEP
        for order, places in enumerate((y, mixed)):
            cos, sin = waves(k, places)
            tables[parity, order] = np.concatenate([cos, sin], axis=0)
    return split_table(tables)


def halves(value):
    high = value.astype(BF16)
    return high, (value - high.astype(F32)).astype(BF16)


def dot(a, b):
    return jnp.dot(a, b, preferred_element_type=F32)


def second_rows(lift, fh, fl, rows, row):
    real_of = [lift(40 * a, 16) for a in range(2)]
    imag_of = [lift(40 * a + 16, 16) for a in range(2)]
    tail_of = [lift(40 * a + 32, 8) for a in range(2)]
    for parity in range(2):

        def fold(pair):
            return pair[0] + pair[1] if parity == 0 else pair[0] - pair[1]

        part = jnp.concatenate([fold(real_of), fold(imag_of)], axis=1)
        tail = fold(tail_of)
        tail = jnp.concatenate([tail, pltpu.roll(tail, 64, 1)], axis=0)
        outs = []
        for order, value in ((0, part), (1, tail)):
            high, low = halves(value)
            a, b = fh[parity, order], fl[parity, order]
            outs.append(dot(a, high) + dot(a, low) + dot(b, high))
        wide, slim = outs
        cos, sin = wide[:160], wide[160:]
        real = cos[:, :128] + sin[:, 128:]
        imag = cos[:, 128:] - sin[:, :128]
        cos, sin = slim[:160], slim[160:]
        tail_real = cos + pltpu.roll(sin, 96, 1)
        tail_imag = cos - pltpu.roll(sin, 32, 1)
        result = jnp.concatenate(
            [real, tail_real[:, :32], imag, tail_imag[:, 32:64], jnp.zeros((160, 64), F32)], axis=1
        )
        if parity == 0:
            at_row = lax.broadcasted_iota(jnp.int32, (160, 384), 0)
            at_col = lax.broadcasted_iota(jnp.int32, (160, 384), 1)
            zero = (at_row == 80) & (at_col == 0) & (row == KEEP)
            result = jnp.where(zero, 0.0, result)
        for place in range(3):
            rows[place, pl.ds(parity, 160, stride=2), :] = result[:, place * 128 : place * 128 + 128]


def exchange_kernel(
    u, v, t, zh, zl, xh, xl, fh, fl, yall, parts,
    fields, zth, ztl, xth, xtl, fth, ftl, stack, held, zbuf, zout, xs, xr, xsm, xrm, dall, rows,
    in_sem, tab_sem, zs_sem, zr_sem, xs_sem, xr_sem, ds_sem, dr_sem, dl_sem, y_sem, p_sem,
):
    field, slab = lax.axis_index("field"), lax.axis_index("slab")
    hi, core = field // 2, field % 2
    lo, plane = slab // 16, slab % 16
    own = hi * 2 + lo

    def peer_x(rel):
        half, side = (hi + rel // 2) % 2, (lo + rel % 2) % 2
        return half, side, {"field": half * 2 + core, "slab": side * 16 + plane}

    def peer_plane(step):
        other = (plane // 4 + step[0]) % 4 * 4 + (plane + step[1]) % 4
        return other, {"field": field, "slab": lo * 16 + other}

    partner = {"field": hi * 2 + (1 - core), "slab": slab}

    def loads(octet):
        return [
            pltpu.make_async_copy(
                ref.at[:, pl.ds(8 * octet, 8), pl.ds(128 * part, 128)],
                fields.at[i, part, octet],
                in_sem.at[octet, i, part],
            )
            for part in range(4)
            for i, ref in enumerate((u, v, t))
        ]

    tables = [
        pltpu.make_async_copy(src, dst, tab_sem.at[i])
        for i, (src, dst) in enumerate(
            ((zh, zth), (zl, ztl), (xh.at[hi], xth), (xl.at[hi], xtl), (fh, fth), (fl, ftl))
        )
    ]
    tables[0].start()
    for load in loads(0):
        load.start()
    for table in tables[1:4]:
        table.start()
    for load in loads(1):
        load.start()
    for table in tables[4:]:
        table.start()

    barrier = pltpu.get_barrier_semaphore()
    pl.semaphore_signal(barrier, 1, device_id=partner, device_id_type=MESH)
    for rel in range(1, 4):
        pl.semaphore_signal(barrier, 1, device_id=peer_x(rel)[2], device_id_type=MESH)

    for step in STEPS:
        pl.semaphore_signal(barrier, 1, device_id=peer_plane(step)[1], device_id_type=MESH)
    pl.semaphore_wait(barrier, 19)

    def z_slot(chunk):
        return jnp.where(chunk < 16, chunk % 4, 4 + chunk % 2)

    def z_copy(chunk):
        return pltpu.make_async_remote_copy(
            src_ref=zout.at[z_slot(chunk)],
            dst_ref=zbuf.at[chunk, :, pl.ds(pl.multiple_of(core * 128, 128), 128), :],
            send_sem=zs_sem.at[chunk],
            recv_sem=zr_sem.at[chunk],
            device_id=partner,
            device_id_type=MESH,
        )

    def put_z(chunk, value):
        rows = pl.ds(pl.multiple_of(core * 128, 128), 128)
        for half in range(2):
            zbuf[chunk, half, rows, :] = value[half * 128 : half * 128 + 128]
            zout[z_slot(chunk), half] = value[256 + half * 128 : 384 + half * 128]
        z_copy(chunk).start()

    flat = fields.reshape(3, 4, 2048, 128)

    def depth_by(table):
        both = dot(stack[...], zth[table])
        return both[:512] + both[512:] + dot(stack[:512], ztl[table])

    def depth_main(y):
        for part in range(4):
            rows = pl.ds((y // 8) * 1024 + y % 8, 128, stride=8)
            values = [flat[i, part, rows, :] for i in range(3)]
            columns = slice(part * 128, part * 128 + 128)
            for product, (a, b) in enumerate(FACTORS):
                high, low = halves(values[a] * values[b])
                row = (product + core) % 2 * 256 + product // 2 * 128
                stack[pl.ds(pl.multiple_of(row, 128), 128), columns] = high
                stack[pl.ds(pl.multiple_of(row + 512, 128), 128), columns] = low

        @pl.when(y >= 4)
        def _():
            z_copy(y - 4).wait_send()

        put_z(y, depth_by(0))

    def depth_tail(y):
        tail = depth_by(1 + y % 2)

        @pl.when(y % 2 == 0)
        def _():
            held[...] = tail

        @pl.when(y % 2 == 1)
        def _():
            @pl.when(y >= 4)
            def _():
                z_copy(16 + y // 2 - 2).wait_send()

            put_z(16 + y // 2, held[...] + tail)

    def first(chunk):
        z_copy(chunk).wait_recv()
        pairs = []
        for half in range(2):
            high, low = halves(zbuf[chunk, half])
            mixed = dot(xth[...], high) + dot(xth[...], low) + dot(xtl[...], high)
            pairs.append((half, mixed[:176], mixed[176:]))
        return pairs

    def rows_at(side, i):
        return 16 * i if side == 1 else 16 * (10 - i)

    def x_copy(rel, y, group):
        half, side, device = peer_x(rel)
        at, count = 32 * STARTS[group], 32 * GROUPS[group]

        def rows(item):
            return pl.ds(pl.multiple_of(item * PITCH + at, 8), count)

        return pltpu.make_async_remote_copy(
            src_ref=xs.at[rows((half * 2 + side) * 16 + y), :],
            dst_ref=xr.at[rows((rel - 1) * 16 + y), :],
            send_sem=xs_sem.at[0, rel - 1, group],
            recv_sem=xr_sem.at[0, rel - 1, group],
            device_id=device,
            device_id_type=MESH,
        )

    def xm_copy(rel, pair, group):
        half, side, device = peer_x(rel)
        at, count = 16 * STARTS[group], 16 * GROUPS[group]

        def rows(item):
            return pl.ds(pl.multiple_of(item * MIX_PITCH + at, 8), count)

        return pltpu.make_async_remote_copy(
            src_ref=xsm.at[rows((half * 2 + side) * 8 + pair), :],
            dst_ref=xrm.at[rows((rel - 1) * 8 + pair), :],
            send_sem=xs_sem.at[1, rel - 1, group],
            recv_sem=xr_sem.at[1, rel - 1, group],
            device_id=device,
            device_id_type=MESH,
        )

    def first_main(y):
        for half, cos, sin in first(y):
            for side in range(2):
                base = ((half * 2 + side) * 16 + y) * PITCH
                sign = 1.0 if side == 1 else -1.0
                real = cos[:, :128] + sign * sin[:, 128:]
                imag = cos[:, 128:] - sign * sin[:, :128]
                for i0, count in zip(STARTS, GROUPS):
                    at = base + 32 * i0
                    for i in range(count):
                        rows = slice(rows_at(side, i0 + i), rows_at(side, i0 + i) + 16)
                        xs[pl.ds(pl.multiple_of(at + 16 * i, 8), 16), :] = real[rows]
                        xs[pl.ds(pl.multiple_of(at + 16 * (count + i), 8), 16), :] = imag[rows]
        for rel in (2, 1, 3):
            x_copy(rel, y, 0).start()

    def first_mix(pair):
        for half, cos, sin in first(16 + pair):
            for side in range(2):
                at = ((half * 2 + side) * 8 + pair) * MIX_PITCH
                sign = 1.0 if side == 1 else -1.0
                value = cos[:, :128] + sign * sin[:, 128:]
                for i in range(10):
                    rows = slice(rows_at(side, i), rows_at(side, i) + 16)
                    xsm[pl.ds(pl.multiple_of(at + 16 * i, 8), 16), :] = value[rows]
        for rel in (2, 1, 3):
            xm_copy(rel, pair, 0).start()

    tables[0].wait()
    for load in loads(0):
        load.wait()
    for table in tables[1:4]:
        table.wait()

    def produce(step, carry):
        @pl.when(step == 8)
        def _():
            for load in loads(1):
                load.wait()

        @pl.when(step < 16)
        def _():
            depth_main(step)

        @pl.when(step != 1)
        def _():
            first_main(jnp.maximum(step - 1, 0))

        @pl.when(step < 16)
        def _():
            depth_tail(step)

        return carry

    lax.fori_loop(0, 17, produce, 0)

    def produce_mix(pair, carry):
        first_mix(pair)
        return carry

    lax.fori_loop(0, 8, produce_mix, 0)

    def send_x(group):
        def go(y, carry):
            for rel in (2, 1, 3):
                x_copy(rel, y, group).start()
            return carry

        lax.fori_loop(0, 16, go, 0)

        def go_mix(pair, carry):
            for rel in (2, 1, 3):
                xm_copy(rel, pair, group).start()
            return carry

        lax.fori_loop(0, 8, go_mix, 0)

    def d_copy(group, device, other):
        span = pl.ds(STARTS[group], GROUPS[group])
        src = dall.at[other, span]
        dst = yall.at[span, pl.ds(pl.multiple_of(plane * 80, 80), 80), :]
        if device is None:
            return pltpu.make_async_copy(src, dst, dl_sem.at[group])
        return pltpu.make_async_remote_copy(
            src_ref=src,
            dst_ref=dst,
            send_sem=ds_sem.at[group],
            recv_sem=dr_sem.at[group],
            device_id=device,
            device_id_type=MESH,
        )

    def turn(group):
        i0, count = STARTS[group], GROUPS[group]
        near, far = lo * 40, (1 - lo) * 40

        def go(r, carry):
            i, place = i0 + r // 16, r % 16
            other = lo * place + (1 - lo) * (15 - place)

            def put(offset, near_value, far_value):
                dall[other, i, pl.ds(pl.multiple_of(near + offset, 8), 8), :] = near_value
                dall[other, i, pl.ds(pl.multiple_of(far + offset, 8), 8), :] = far_value

            for part in range(2):
                for octet in range(2):
                    base = octet * 8 * PITCH + 32 * i0 + part * 16 * count + r

                    def take(ref, item):
                        return ref[pl.ds(item * 16 * PITCH + base, 8, stride=PITCH), :]

                    put(part * 16 + octet * 8, take(xs, own) + take(xr, 1), take(xr, 0) + take(xr, 2))

            def take_mix(ref, item):
                return ref[pl.ds(item * 8 * MIX_PITCH + 16 * i0 + r, 8, stride=MIX_PITCH), :]

            put(32, take_mix(xsm, own) + take_mix(xrm, 1), take_mix(xrm, 0) + take_mix(xrm, 2))
            return carry

        lax.fori_loop(0, 16 * count, go, 0)

    def x_wait(group, sem):
        main = xr.at[pl.ds(0, 512 * GROUPS[group]), :]
        mix = xrm.at[pl.ds(0, 128 * GROUPS[group]), :]
        for rel in range(3):
            pltpu.make_async_copy(main, main, sem.at[0, rel, group]).wait()
            pltpu.make_async_copy(mix, mix, sem.at[1, rel, group]).wait()

    lines = fields.reshape(24576, 128)

    def y_load(i):
        return pltpu.make_async_copy(
            yall.at[i], lines.at[pl.ds(pl.multiple_of(i * 1280, 1280), 1280), :], y_sem.at[i]
        )

    def part_copy(i):
        return pltpu.make_async_copy(rows.at[i % 2], parts.at[i], p_sem.at[i])

    def second(group):
        whole = dall.at[pl.ds(0, 15), pl.ds(0, GROUPS[group])]
        pltpu.make_async_copy(whole, whole, dr_sem.at[group]).wait()
        d_copy(group, None, plane).wait()
        first_i, last_i = STARTS[group], STARTS[group] + GROUPS[group]
        for i in range(first_i, last_i):
            y_load(i).start()

        def go(i, carry):
            y_load(i).wait()

            @pl.when(i >= 2)
            def _():
                part_copy(i - 2).wait()

            def lift(offset, count):
                return jnp.concatenate(
                    [
                        lines[pl.ds(pl.multiple_of(i * 1280 + 80 * j + offset, 8), count), :]
                        for j in range(16)
                    ],
                    axis=0,
                )

            second_rows(lift, fth, ftl, rows.at[i % 2], slab * 10 + i)
            part_copy(i).start()
            return carry

        lax.fori_loop(first_i, last_i, go, 0)

    for group in range(len(GROUPS)):
        if group + 1 < len(GROUPS):
            send_x(group + 1)
        x_wait(group, xr_sem)
        turn(group)

        for step in STEPS:
            other, device = peer_plane(step)
            d_copy(group, device, other).start()
        d_copy(group, None, plane).start()
        if group == 0:
            for table in tables[4:]:
                table.wait()
        else:
            second(group - 1)

    def z_left(chunk, carry):
        z_copy(chunk).wait_send()
        return carry

    lax.fori_loop(12, 16, z_left, 0)
    lax.fori_loop(22, 24, z_left, 0)
    for group in range(len(GROUPS)):
        x_wait(group, xs_sem)
    second(len(GROUPS) - 1)
    for group in range(len(GROUPS)):
        whole = dall.at[pl.ds(0, 15), pl.ds(0, GROUPS[group])]
        pltpu.make_async_copy(whole, whole, ds_sem.at[group]).wait()
    part_copy(8).wait()
    part_copy(9).wait()


def exchange(u, v, t):
    zh, zl = depth_tables()
    xh, xl = first_tables()
    fh, fl = second_tables()
    groups = len(GROUPS)
    any_space = pl.BlockSpec(memory_space=pl.ANY)
    return pl.pallas_call(
        exchange_kernel,
        out_shape=(
            jax.ShapeDtypeStruct((10, 1280, 128), F32),
            jax.ShapeDtypeStruct((10, 3, 320, 128), F32),
        ),
        in_specs=[any_space] * 9,
        out_specs=(any_space, any_space),
        scratch_shapes=[
            pltpu.VMEM((3, 4, 2, 128, 8, 128), F32),
            pltpu.VMEM((3, 512, 256), BF16),
            pltpu.VMEM((3, 512, 256), BF16),
            pltpu.VMEM((352, 256), BF16),
            pltpu.VMEM((352, 256), BF16),
            pltpu.VMEM((2, 2, 320, 256), BF16),
            pltpu.VMEM((2, 2, 320, 256), BF16),
            pltpu.VMEM((1024, 512), BF16),
            pltpu.VMEM((512, 256), F32),
            pltpu.VMEM((24, 2, 256, 256), F32),
            pltpu.VMEM((6, 2, 128, 256), F32),
            pltpu.VMEM((4 * 16 * PITCH, 128), F32),
            pltpu.VMEM((3 * 16 * PITCH, 128), F32),
            pltpu.VMEM((4 * 8 * MIX_PITCH, 128), F32),
            pltpu.VMEM((3 * 8 * MIX_PITCH, 128), F32),
            pltpu.VMEM((16, 10, 80, 128), F32),
            pltpu.VMEM((2, 3, 320, 128), F32),
            pltpu.SemaphoreType.DMA((2, 3, 4)),
            pltpu.SemaphoreType.DMA((6,)),
            pltpu.SemaphoreType.DMA((24,)),
            pltpu.SemaphoreType.DMA((24,)),
            pltpu.SemaphoreType.DMA((2, 3, groups)),
            pltpu.SemaphoreType.DMA((2, 3, groups)),
            pltpu.SemaphoreType.DMA((groups,)),
            pltpu.SemaphoreType.DMA((groups,)),
            pltpu.SemaphoreType.DMA((groups,)),
            pltpu.SemaphoreType.DMA((10,)),
            pltpu.SemaphoreType.DMA((10,)),
        ],
        compiler_params=pltpu.CompilerParams(
            collective_id=0, has_side_effects=True, vmem_limit_bytes=67043328
        ),
        name="exchange",
    )(u, v, t, zh, zl, xh, xl, fh, fl)


def lay_out_kernel(parts, out):
    for i in range(2):
        out[0, i, :, :128] = parts[i, 0]
        out[0, i, :, 128:256] = parts[i, 1]
        out[0, i, :, 256:] = parts[i, 2, :, :64]


def lay_out(parts):
    return pl.pallas_call(
        lay_out_kernel,
        grid=(5,),
        out_shape=jax.ShapeDtypeStruct((1, 10, 320, 320), F32),
        in_specs=[pl.BlockSpec((2, 3, 320, 128), lambda i: (i, 0, 0, 0))],
        out_specs=pl.BlockSpec((1, 2, 320, 320), lambda i: (0, i, 0, 0)),
        compiler_params=pltpu.CompilerParams(dimension_semantics=("arbitrary",)),
        name="lay_out",
    )(parts)


def shards(velocity_u, velocity_v, scalar_theta):
    return lay_out(exchange(velocity_u, velocity_v, scalar_theta)[1])


def solution(mesh):
    spec = P("field", "slab", None)
    return jax.shard_map(
        shards,
        mesh=mesh,
        in_specs=(spec, spec, spec),
        out_specs=P("field", "slab", None, None),
        check_vma=False,
    )
```

time: 401 us -> 181 us (0.45)
  the two profiles are of different devices: /device:TPU:22 before, /device:TPU:0 now
where the time goes in v2:
time: 181 us
  Pallas kernels  181 us (100%)
    pallas_call x1, Pallas kernels, exchange(): pl.pallas_call(exchange_kernel, out_shape=(jax.ShapeDtypeStruct((10, 1280...  174 us
    pallas_call x1, Pallas kernels, lay_out(): pl.pallas_call(lay_out_kernel, grid=(5,), out_shape=jax.ShapeDtypeStruct(...  6.29 us

profile of v2, /device:TPU:0, one launch (start us, length us, event | category | flops | bytes accessed | tf_op | source)
XLA Modules:
  0.0 180.6 jit_solution(8780505039268113563)
XLA Ops:
  0.0 174.3 %exchange.1 = (f32[10,1280,128]{2,1,0:T(8,128)}, f32[10,3,320,128]{3,2,1,0:T(8,128)}) custom-call(f32[128,16,512]{2,1,0:T(8,128)} %u.1, f32[128,16,512]{2,1,0:T(8,128)} %v.1, f32[128,16,512]{2,1,0:T(8,128)} %t.1, bf16[3,512,256]{2,1,0:T(8,128)(2,1)} %constant.12.clone.zh, bf16[3,512,256]{2,1,0:T(8,128)(2,1)} %constant.13.clone.zl, ...), custom_call_target="tpu_custom_call" | custom-call | tf_op jit(solution)/shard_map/exchange/pallas_call | solution.py:483
  174.3 6.3 %lay_out.1 = f32[1,10,320,320]{3,2,1,0:T(8,128)} custom-call(f32[10,3,320,128]{3,2,1,0:T(8,128)} %get-tuple-element.6.parts), custom_call_target="tpu_custom_call" | custom-call | tf_op jit(solution)/shard_map/lay_out/pallas_call | solution.py:536

commit v3 on v2

--- a/solution.py
+++ b/solution.py
@@ -13,13 +13,16 @@
 MESH = pl.DeviceIdType.MESH
 F32 = jnp.float32
 BF16 = jnp.bfloat16
-GROUPS = (4, 3, 1, 1, 1)
-STARTS = (0, 4, 7, 8, 9)
+GROUPS = (3, 3, 2, 1, 1)
+STARTS = (0, 3, 6, 8, 9)
+LAST = 4
+PHASES = ((0, 0, 2, True), (1, 0, 2, True), (2, 0, 2, True), (3, 0, 2, True), (4, 0, 1, False), (4, 1, 2, False), (4, 2, 2, True))
 STEPS = (
     ((0, 1), (1, 0), (0, 3), (3, 0), (1, 1), (3, 3), (1, 3), (3, 1))
     + ((2, 1), (2, 3), (0, 2), (2, 0), (2, 2))
     + ((1, 2), (3, 2))
 )
+EARLY = 8
 PITCH = 328
 MIX_PITCH = 168
 FACTORS = ((0, 0), (1, 1), (0, 1), (0, 2))
@@ -81,9 +84,9 @@
 
 
 def second_rows(lift, fh, fl, rows, row):
-    real_of = [lift(40 * a, 16) for a in range(2)]
-    imag_of = [lift(40 * a + 16, 16) for a in range(2)]
-    tail_of = [lift(40 * a + 32, 8) for a in range(2)]
+    real_of = [lift((16 * a, 32 + 16 * a)) for a in range(2)]
+    imag_of = [lift((16 * a + 8, 40 + 16 * a)) for a in range(2)]
+    tail_of = [lift((64 + 8 * a,)) for a in range(2)]
     for parity in range(2):
 
         def fold(pair):
@@ -118,7 +121,7 @@
 
 def exchange_kernel(
     u, v, t, zh, zl, xh, xl, fh, fl, yall, parts,
-    fields, zth, ztl, xth, xtl, fth, ftl, stack, held, zbuf, zout, xs, xr, xsm, xrm, dall, rows,
+    fields, zth, ztl, xth, xtl, fth, ftl, stack, held, zbuf, zout, xs, xr, xsm, xrm, dall, ylast, rows,
     in_sem, tab_sem, zs_sem, zr_sem, xs_sem, xr_sem, ds_sem, dr_sem, dl_sem, y_sem, p_sem,
 ):
     field, slab = lax.axis_index("field"), lax.axis_index("slab")
@@ -150,17 +153,18 @@
     tables = [
         pltpu.make_async_copy(src, dst, tab_sem.at[i])
         for i, (src, dst) in enumerate(
-            ((zh, zth), (zl, ztl), (xh.at[hi], xth), (xl.at[hi], xtl), (fh, fth), (fl, ftl))
+            (
+                (zh.at[0], zth.at[0]), (zl.at[0], ztl.at[0]), (xh.at[hi], xth), (xl.at[hi], xtl),
+                (zh.at[pl.ds(1, 2)], zth.at[pl.ds(1, 2)]), (zl.at[pl.ds(1, 2)], ztl.at[pl.ds(1, 2)]),
+                (fh, fth), (fl, ftl),
+            )
         )
     ]
     tables[0].start()
+    tables[1].start()
     for load in loads(0):
         load.start()
-    for table in tables[1:4]:
-        table.start()
-    for load in loads(1):
-        load.start()
-    for table in tables[4:]:
+    for table in tables[2:4]:
         table.start()
 
     barrier = pltpu.get_barrier_semaphore()
@@ -242,8 +246,9 @@
     def rows_at(side, i):
         return 16 * i if side == 1 else 16 * (10 - i)
 
-    def x_copy(rel, y, group):
+    def x_copy(rel, y, phase):
         half, side, device = peer_x(rel)
+        group = PHASES[phase][0]
         at, count = 32 * STARTS[group], 32 * GROUPS[group]
 
         def rows(item):
@@ -252,14 +257,15 @@
         return pltpu.make_async_remote_copy(
             src_ref=xs.at[rows((half * 2 + side) * 16 + y), :],
             dst_ref=xr.at[rows((rel - 1) * 16 + y), :],
-            send_sem=xs_sem.at[0, rel - 1, group],
-            recv_sem=xr_sem.at[0, rel - 1, group],
+            send_sem=xs_sem.at[0, rel - 1, phase],
+            recv_sem=xr_sem.at[0, rel - 1, phase],
             device_id=device,
             device_id_type=MESH,
         )
 
-    def xm_copy(rel, pair, group):
+    def xm_copy(rel, pair, phase):
         half, side, device = peer_x(rel)
+        group = PHASES[phase][0]
         at, count = 16 * STARTS[group], 16 * GROUPS[group]
 
         def rows(item):
@@ -268,8 +274,8 @@
         return pltpu.make_async_remote_copy(
             src_ref=xsm.at[rows((half * 2 + side) * 8 + pair), :],
             dst_ref=xrm.at[rows((rel - 1) * 8 + pair), :],
-            send_sem=xs_sem.at[1, rel - 1, group],
-            recv_sem=xr_sem.at[1, rel - 1, group],
+            send_sem=xs_sem.at[1, rel - 1, phase],
+            recv_sem=xr_sem.at[1, rel - 1, phase],
             device_id=device,
             device_id_type=MESH,
         )
@@ -290,6 +296,11 @@
         for rel in (2, 1, 3):
             x_copy(rel, y, 0).start()
 
+        @pl.when(y < EARLY)
+        def _():
+            for rel in (2, 1, 3):
+                x_copy(rel, y, 1).start()
+
     def first_mix(pair):
         for half, cos, sin in first(16 + pair):
             for side in range(2):
@@ -307,6 +318,12 @@
         load.wait()
     for table in tables[1:4]:
         table.wait()
+    for table in tables[4:6]:
+        table.start()
+    for load in loads(1):
+        load.start()
+    for table in tables[6:]:
+        table.start()
 
     def produce(step, carry):
         @pl.when(step == 8)
@@ -321,6 +338,11 @@
         @pl.when(step != 1)
         def _():
             first_main(jnp.maximum(step - 1, 0))
+
+        @pl.when(step == 0)
+        def _():
+            for table in tables[4:6]:
+                table.wait()
 
         @pl.when(step < 16)
         def _():
@@ -336,71 +358,94 @@
 
     lax.fori_loop(0, 8, produce_mix, 0)
 
-    def send_x(group):
+    def send_x(phase):
+        group, octet, until, with_mix = PHASES[phase]
+
         def go(y, carry):
             for rel in (2, 1, 3):
-                x_copy(rel, y, group).start()
+                x_copy(rel, y, phase).start()
             return carry
 
-        lax.fori_loop(0, 16, go, 0)
+        if until > octet:
+            lax.fori_loop(EARLY if phase == 1 else 8 * octet, 8 * until, go, 0)
 
         def go_mix(pair, carry):
             for rel in (2, 1, 3):
-                xm_copy(rel, pair, group).start()
+                xm_copy(rel, pair, phase).start()
             return carry
 
-        lax.fori_loop(0, 8, go_mix, 0)
-
-    def d_copy(group, device, other):
-        span = pl.ds(STARTS[group], GROUPS[group])
-        src = dall.at[other, span]
-        dst = yall.at[span, pl.ds(pl.multiple_of(plane * 80, 80), 80), :]
+        if with_mix:
+            lax.fori_loop(0, 8, go_mix, 0)
+
+    def d_span(phase):
+        group, octet, until, with_mix = PHASES[phase]
+        first_row, last_row = 32 * octet, 80 if with_mix else 32 * until
+        return pl.ds(STARTS[group], GROUPS[group]), first_row, last_row - first_row
+
+    def d_copy(phase, device, other):
+        span, row, count = d_span(phase)
+        src = dall.at[other, span, pl.ds(row, count)]
+        place = pl.ds(pl.multiple_of(plane * 80 + row, 8), count)
+        if PHASES[phase][0] == LAST:
+            dst = ylast.at[:, place, :]
+        else:
+            dst = yall.at[span, place, :]
         if device is None:
-            return pltpu.make_async_copy(src, dst, dl_sem.at[group])
+            return pltpu.make_async_copy(src, dst, dl_sem.at[phase])
         return pltpu.make_async_remote_copy(
             src_ref=src,
             dst_ref=dst,
-            send_sem=ds_sem.at[group],
-            recv_sem=dr_sem.at[group],
+            send_sem=ds_sem.at[phase],
+            recv_sem=dr_sem.at[phase],
             device_id=device,
             device_id_type=MESH,
         )
 
-    def turn(group):
+    def d_wait(phase, sem):
+        span, row, count = d_span(phase)
+        whole = dall.at[pl.ds(0, 15), span, pl.ds(row, count)]
+        pltpu.make_async_copy(whole, whole, sem.at[phase]).wait()
+
+    def turn(phase):
+        group, first_octet, until, with_mix = PHASES[phase]
         i0, count = STARTS[group], GROUPS[group]
-        near, far = lo * 40, (1 - lo) * 40
 
         def go(r, carry):
             i, place = i0 + r // 16, r % 16
             other = lo * place + (1 - lo) * (15 - place)
 
-            def put(offset, near_value, far_value):
-                dall[other, i, pl.ds(pl.multiple_of(near + offset, 8), 8), :] = near_value
-                dall[other, i, pl.ds(pl.multiple_of(far + offset, 8), 8), :] = far_value
-
-            for part in range(2):
-                for octet in range(2):
+            def put(octet, offset, near_value, far_value):
+                pitch, base = (16, 16, 8)[octet], 32 * octet + offset
+                dall[other, i, pl.ds(pl.multiple_of(lo * pitch + base, 8), 8), :] = near_value
+                dall[other, i, pl.ds(pl.multiple_of((1 - lo) * pitch + base, 8), 8), :] = far_value
+
+            for octet in range(first_octet, until):
+                for part in range(2):
                     base = octet * 8 * PITCH + 32 * i0 + part * 16 * count + r
 
                     def take(ref, item):
                         return ref[pl.ds(item * 16 * PITCH + base, 8, stride=PITCH), :]
 
-                    put(part * 16 + octet * 8, take(xs, own) + take(xr, 1), take(xr, 0) + take(xr, 2))
+                    put(octet, part * 8, take(xs, own) + take(xr, 1), take(xr, 0) + take(xr, 2))
 
             def take_mix(ref, item):
                 return ref[pl.ds(item * 8 * MIX_PITCH + 16 * i0 + r, 8, stride=MIX_PITCH), :]
 
-            put(32, take_mix(xsm, own) + take_mix(xrm, 1), take_mix(xrm, 0) + take_mix(xrm, 2))
+            if with_mix:
+                put(2, 0, take_mix(xsm, own) + take_mix(xrm, 1), take_mix(xrm, 0) + take_mix(xrm, 2))
             return carry
 
         lax.fori_loop(0, 16 * count, go, 0)
 
-    def x_wait(group, sem):
-        main = xr.at[pl.ds(0, 512 * GROUPS[group]), :]
+    def x_wait(phase, sem):
+        group, octet, until, with_mix = PHASES[phase]
+        main = xr.at[pl.ds(0, 256 * (until - octet) * GROUPS[group]), :]
         mix = xrm.at[pl.ds(0, 128 * GROUPS[group]), :]
         for rel in range(3):
-            pltpu.make_async_copy(main, main, sem.at[0, rel, group]).wait()
-            pltpu.make_async_copy(mix, mix, sem.at[1, rel, group]).wait()
+            if until > octet:
+                pltpu.make_async_copy(main, main, sem.at[0, rel, phase]).wait()
+            if with_mix:
+                pltpu.make_async_copy(mix, mix, sem.at[1, rel, phase]).wait()
 
     lines = fields.reshape(24576, 128)
 
@@ -413,25 +458,31 @@
         return pltpu.make_async_copy(rows.at[i % 2], parts.at[i], p_sem.at[i])
 
     def second(group):
-        whole = dall.at[pl.ds(0, 15), pl.ds(0, GROUPS[group])]
-        pltpu.make_async_copy(whole, whole, dr_sem.at[group]).wait()
-        d_copy(group, None, plane).wait()
+        for phase in range(len(PHASES)):
+            if PHASES[phase][0] == group:
+                d_wait(phase, dr_sem)
+                d_copy(phase, None, plane).wait()
         first_i, last_i = STARTS[group], STARTS[group] + GROUPS[group]
-        for i in range(first_i, last_i):
-            y_load(i).start()
+        if group < LAST:
+            for i in range(first_i, last_i):
+                y_load(i).start()
 
         def go(i, carry):
-            y_load(i).wait()
+            if group < LAST:
+                y_load(i).wait()
 
             @pl.when(i >= 2)
             def _():
                 part_copy(i - 2).wait()
 
-            def lift(offset, count):
+            def lift(offsets):
                 return jnp.concatenate(
                     [
-                        lines[pl.ds(pl.multiple_of(i * 1280 + 80 * j + offset, 8), count), :]
+                        lines[pl.ds(pl.multiple_of(i * 1280 + 80 * j + offset, 8), 8), :]
+                        if group < LAST
+                        else ylast[0, 80 * j + offset : 80 * j + offset + 8, :]
                         for j in range(16)
+                        for offset in offsets
                     ],
                     axis=0,
                 )
@@ -442,21 +493,20 @@
 
         lax.fori_loop(first_i, last_i, go, 0)
 
-    for group in range(len(GROUPS)):
-        if group + 1 < len(GROUPS):
-            send_x(group + 1)
-        x_wait(group, xr_sem)
-        turn(group)
-
+    for phase in range(len(PHASES)):
+        if phase + 1 < len(PHASES):
+            send_x(phase + 1)
+        x_wait(phase, xr_sem)
+        turn(phase)
         for step in STEPS:
             other, device = peer_plane(step)
-            d_copy(group, device, other).start()
-        d_copy(group, None, plane).start()
-        if group == 0:
-            for table in tables[4:]:
+            d_copy(phase, device, other).start()
+        d_copy(phase, None, plane).start()
+        if phase == 0:
+            for table in tables[6:]:
                 table.wait()
-        else:
-            second(group - 1)
+        elif phase < len(GROUPS):
+            second(phase - 1)
 
     def z_left(chunk, carry):
         z_copy(chunk).wait_send()
@@ -464,12 +514,11 @@
 
     lax.fori_loop(12, 16, z_left, 0)
     lax.fori_loop(22, 24, z_left, 0)
-    for group in range(len(GROUPS)):
-        x_wait(group, xs_sem)
+    for phase in range(len(PHASES)):
+        x_wait(phase, xs_sem)
     second(len(GROUPS) - 1)
-    for group in range(len(GROUPS)):
-        whole = dall.at[pl.ds(0, 15), pl.ds(0, GROUPS[group])]
-        pltpu.make_async_copy(whole, whole, ds_sem.at[group]).wait()
+    for phase in range(len(PHASES)):
+        d_wait(phase, ds_sem)
     part_copy(8).wait()
     part_copy(9).wait()
 
@@ -478,12 +527,12 @@
     zh, zl = depth_tables()
     xh, xl = first_tables()
     fh, fl = second_tables()
-    groups = len(GROUPS)
+    phases = len(PHASES)
     any_space = pl.BlockSpec(memory_space=pl.ANY)
     return pl.pallas_call(
         exchange_kernel,
         out_shape=(
-            jax.ShapeDtypeStruct((10, 1280, 128), F32),
+            jax.ShapeDtypeStruct((9, 1280, 128), F32),
             jax.ShapeDtypeStruct((10, 3, 320, 128), F32),
         ),
         in_specs=[any_space] * 9,
@@ -505,16 +554,17 @@
             pltpu.VMEM((4 * 8 * MIX_PITCH, 128), F32),
             pltpu.VMEM((3 * 8 * MIX_PITCH, 128), F32),
             pltpu.VMEM((16, 10, 80, 128), F32),
+            pltpu.VMEM((1, 1280, 128), F32),
             pltpu.VMEM((2, 3, 320, 128), F32),
             pltpu.SemaphoreType.DMA((2, 3, 4)),
-            pltpu.SemaphoreType.DMA((6,)),
+            pltpu.SemaphoreType.DMA((8,)),
             pltpu.SemaphoreType.DMA((24,)),
             pltpu.SemaphoreType.DMA((24,)),
-            pltpu.SemaphoreType.DMA((2, 3, groups)),
-            pltpu.SemaphoreType.DMA((2, 3, groups)),
-            pltpu.SemaphoreType.DMA((groups,)),
-            pltpu.SemaphoreType.DMA((groups,)),
-            pltpu.SemaphoreType.DMA((groups,)),
+            pltpu.SemaphoreType.DMA((2, 3, phases)),
+            pltpu.SemaphoreType.DMA((2, 3, phases)),
+            pltpu.SemaphoreType.DMA((phases,)),
+            pltpu.SemaphoreType.DMA((phases,)),
+            pltpu.SemaphoreType.DMA((phases,)),
             pltpu.SemaphoreType.DMA((10,)),
             pltpu.SemaphoreType.DMA((10,)),
         ],
@@ -526,7 +576,7 @@
 
 
 def lay_out_kernel(parts, out):
-    for i in range(2):
+    for i in range(5):
         out[0, i, :, :128] = parts[i, 0]
         out[0, i, :, 128:256] = parts[i, 1]
         out[0, i, :, 256:] = parts[i, 2, :, :64]
@@ -535,10 +585,10 @@
 def lay_out(parts):
     return pl.pallas_call(
         lay_out_kernel,
-        grid=(5,),
+        grid=(2,),
         out_shape=jax.ShapeDtypeStruct((1, 10, 320, 320), F32),
-        in_specs=[pl.BlockSpec((2, 3, 320, 128), lambda i: (i, 0, 0, 0))],
-        out_specs=pl.BlockSpec((1, 2, 320, 320), lambda i: (0, i, 0, 0)),
+        in_specs=[pl.BlockSpec((5, 3, 320, 128), lambda i: (i, 0, 0, 0))],
+        out_specs=pl.BlockSpec((1, 5, 320, 320), lambda i: (0, i, 0, 0)),
         compiler_params=pltpu.CompilerParams(dimension_semantics=("arbitrary",)),
         name="lay_out",
     )(parts)

time: 181 us -> 172 us (0.950)
  Pallas kernels: 181 us -> 172 us
    pallas_call x2, Pallas kernels: 181 us -> 172 us  [the longest x1 168 us: exchange(): pl.pallas_call(exchange_kernel, out_shape=(jax.ShapeDtypeStruct((9, 1280,...]
where the time goes in v3:
time: 172 us
  Pallas kernels  172 us (100%)
    pallas_call x1, Pallas kernels, exchange(): pl.pallas_call(exchange_kernel, out_shape=(jax.ShapeDtypeStruct((9, 1280,...  168 us
    pallas_call x1, Pallas kernels, lay_out(): pl.pallas_call(lay_out_kernel, grid=(2,), out_shape=jax.ShapeDtypeStruct(...  4.11 us

profile of v3, /device:TPU:0, one launch (start us, length us, event | category | flops | bytes accessed | tf_op | source)
XLA Modules:
  0.0 172.2 jit_solution(15994258242586331916)
XLA Ops:
  0.0 168.1 %exchange.1 = (f32[9,1280,128]{2,1,0:T(8,128)}, f32[10,3,320,128]{3,2,1,0:T(8,128)}) custom-call(f32[128,16,512]{2,1,0:T(8,128)} %u.1, f32[128,16,512]{2,1,0:T(8,128)} %v.1, f32[128,16,512]{2,1,0:T(8,128)} %t.1, bf16[3,512,256]{2,1,0:T(8,128)(2,1)} %constant.12.clone.zh, bf16[3,512,256]{2,1,0:T(8,128)(2,1)} %constant.13.clone.zl, ...), custom_call_target="tpu_custom_call" | custom-call | tf_op jit(solution)/shard_map/exchange/pallas_call | solution.py:532
  168.1 4.1 %lay_out.1 = f32[1,10,320,320]{3,2,1,0:T(8,128)} custom-call(f32[10,3,320,128]{3,2,1,0:T(8,128)} %get-tuple-element.6.parts), custom_call_target="tpu_custom_call" | custom-call | tf_op jit(solution)/shard_map/lay_out/pallas_call | solution.py:586

commit v4 on v3

--- a/solution.py
+++ b/solution.py
@@ -13,10 +13,13 @@
 MESH = pl.DeviceIdType.MESH
 F32 = jnp.float32
 BF16 = jnp.bfloat16
-GROUPS = (3, 3, 2, 1, 1)
-STARTS = (0, 3, 6, 8, 9)
-LAST = 4
-PHASES = ((0, 0, 2, True), (1, 0, 2, True), (2, 0, 2, True), (3, 0, 2, True), (4, 0, 1, False), (4, 1, 2, False), (4, 2, 2, True))
+GROUPS = (3, 2, 2, 1, 1, 1)
+STARTS = (0, 3, 5, 7, 8, 9)
+LAST = 5
+PHASES = (
+    ((0, 0, 2, True), (1, 0, 2, True), (2, 0, 2, True), (3, 0, 2, True), (4, 0, 2, True))
+    + ((5, 0, 1, False), (5, 1, 2, False), (5, 2, 2, True))
+)
 STEPS = (
     ((0, 1), (1, 0), (0, 3), (3, 0), (1, 1), (3, 3), (1, 3), (3, 1))
     + ((2, 1), (2, 3), (0, 2), (2, 0), (2, 2))
@@ -293,12 +296,12 @@
                         rows = slice(rows_at(side, i0 + i), rows_at(side, i0 + i) + 16)
                         xs[pl.ds(pl.multiple_of(at + 16 * i, 8), 16), :] = real[rows]
                         xs[pl.ds(pl.multiple_of(at + 16 * (count + i), 8), 16), :] = imag[rows]
-        for rel in (2, 1, 3):
+        for rel in (1, 3, 2):
             x_copy(rel, y, 0).start()
 
         @pl.when(y < EARLY)
         def _():
-            for rel in (2, 1, 3):
+            for rel in (1, 3, 2):
                 x_copy(rel, y, 1).start()
 
     def first_mix(pair):
@@ -310,7 +313,7 @@
                 for i in range(10):
                     rows = slice(rows_at(side, i), rows_at(side, i) + 16)
                     xsm[pl.ds(pl.multiple_of(at + 16 * i, 8), 16), :] = value[rows]
-        for rel in (2, 1, 3):
+        for rel in (1, 3, 2):
             xm_copy(rel, pair, 0).start()
 
     tables[0].wait()
@@ -362,7 +365,7 @@
         group, octet, until, with_mix = PHASES[phase]
 
         def go(y, carry):
-            for rel in (2, 1, 3):
+            for rel in (1, 3, 2):
                 x_copy(rel, y, phase).start()
             return carry
 
@@ -370,7 +373,7 @@
             lax.fori_loop(EARLY if phase == 1 else 8 * octet, 8 * until, go, 0)
 
         def go_mix(pair, carry):
-            for rel in (2, 1, 3):
+            for rel in (1, 3, 2):
                 xm_copy(rel, pair, phase).start()
             return carry
 
@@ -505,8 +508,8 @@
         if phase == 0:
             for table in tables[6:]:
                 table.wait()
-        elif phase < len(GROUPS):
-            second(phase - 1)
+        elif 2 <= phase <= LAST + 1:
+            second(phase - 2)
 
     def z_left(chunk, carry):
         z_copy(chunk).wait_send()

time: 172 us -> 168 us (0.977)
  Pallas kernels: 172 us -> 168 us
    pallas_call x1, Pallas kernels: 168 us -> 164 us  [exchange(): pl.pallas_call(exchange_kernel, out_shape=(jax.ShapeDtypeStruct((9, 1280,...]
where the time goes in v4:
time: 168 us
  Pallas kernels  168 us (100%)
    pallas_call x1, Pallas kernels, exchange(): pl.pallas_call(exchange_kernel, out_shape=(jax.ShapeDtypeStruct((9, 1280,...  164 us
    pallas_call x1, Pallas kernels, lay_out(): pl.pallas_call(lay_out_kernel, grid=(2,), out_shape=jax.ShapeDtypeStruct(...  4.11 us

profile of v4, /device:TPU:0, one launch (start us, length us, event | category | flops | bytes accessed | tf_op | source)
XLA Modules:
  0.0 167.6 jit_solution(14378610640987882043)
XLA Ops:
  0.0 163.5 %exchange.1 = (f32[9,1280,128]{2,1,0:T(8,128)}, f32[10,3,320,128]{3,2,1,0:T(8,128)}) custom-call(f32[128,16,512]{2,1,0:T(8,128)} %u.1, f32[128,16,512]{2,1,0:T(8,128)} %v.1, f32[128,16,512]{2,1,0:T(8,128)} %t.1, bf16[3,512,256]{2,1,0:T(8,128)(2,1)} %constant.12.clone.zh, bf16[3,512,256]{2,1,0:T(8,128)(2,1)} %constant.13.clone.zl, ...), custom_call_target="tpu_custom_call" | custom-call | tf_op jit(solution)/shard_map/exchange/pallas_call | solution.py:535
  163.5 4.1 %lay_out.1 = f32[1,10,320,320]{3,2,1,0:T(8,128)} custom-call(f32[10,3,320,128]{3,2,1,0:T(8,128)} %get-tuple-element.6.parts), custom_call_target="tpu_custom_call" | custom-call | tf_op jit(solution)/shard_map/lay_out/pallas_call | solution.py:589

commit v5 on v4

--- a/solution.py
+++ b/solution.py
@@ -25,7 +25,7 @@
     + ((2, 1), (2, 3), (0, 2), (2, 0), (2, 2))
     + ((1, 2), (3, 2))
 )
-EARLY = 8
+EARLY = 4
 PITCH = 328
 MIX_PITCH = 168
 FACTORS = ((0, 0), (1, 1), (0, 1), (0, 2))
@@ -511,6 +511,8 @@
         elif 2 <= phase <= LAST + 1:
             second(phase - 2)
 
+    second(LAST)
+
     def z_left(chunk, carry):
         z_copy(chunk).wait_send()
         return carry
@@ -519,7 +521,6 @@
     lax.fori_loop(22, 24, z_left, 0)
     for phase in range(len(PHASES)):
         x_wait(phase, xs_sem)
-    second(len(GROUPS) - 1)
     for phase in range(len(PHASES)):
         d_wait(phase, ds_sem)
     part_copy(8).wait()

time: 168 us -> 168 us (level)
  no operation moved by 1% of the time
where the time goes in v5:
time: 168 us
  Pallas kernels  168 us (100%)
    pallas_call x1, Pallas kernels, exchange(): pl.pallas_call(exchange_kernel, out_shape=(jax.ShapeDtypeStruct((9, 1280,...  164 us
    pallas_call x1, Pallas kernels, lay_out(): pl.pallas_call(lay_out_kernel, grid=(2,), out_shape=jax.ShapeDtypeStruct(...  4.11 us

profile of v5, /device:TPU:0, one launch (start us, length us, event | category | flops | bytes accessed | tf_op | source)
XLA Modules:
  0.0 167.6 jit_solution(17526585721309488329)
XLA Ops:
  0.0 163.5 %exchange.1 = (f32[9,1280,128]{2,1,0:T(8,128)}, f32[10,3,320,128]{3,2,1,0:T(8,128)}) custom-call(f32[128,16,512]{2,1,0:T(8,128)} %u.1, f32[128,16,512]{2,1,0:T(8,128)} %v.1, f32[128,16,512]{2,1,0:T(8,128)} %t.1, bf16[3,512,256]{2,1,0:T(8,128)(2,1)} %constant.12.clone.zh, bf16[3,512,256]{2,1,0:T(8,128)(2,1)} %constant.13.clone.zl, ...), custom_call_target="tpu_custom_call" | custom-call | tf_op jit(solution)/shard_map/exchange/pallas_call | solution.py:536
  163.5 4.1 %lay_out.1 = f32[1,10,320,320]{3,2,1,0:T(8,128)} custom-call(f32[10,3,320,128]{3,2,1,0:T(8,128)} %get-tuple-element.6.parts), custom_call_target="tpu_custom_call" | custom-call | tf_op jit(solution)/shard_map/lay_out/pallas_call | solution.py:590
